TPU v7x, 32 devices: a whole 2x2x4 slice. The times are simulated.
32 devices in a mesh: dp: 8 (over z, x), tp: 4 (over y, core).
Axes of the slice: x: 2, y: 2, z: 4, core: 2. Of those that a mesh axis runs over, the one named last changes fastest.
Arguments:
- queries: bfloat16 [512, 73728], P('dp', 'tp'), may hold values from -32 to 32
- prefix_cache: bfloat16 [8, 576, 1024], P('dp', None, 'tp'), may hold values from -12 to 12
- suffix_cache: bfloat16 [512, 576, 128], P('dp'), may hold values from -48 to 48
- w_uv: bfloat16 [128, 512, 128], P('tp'), may hold values from -1 to 1
- fork_prompt: int32 [512, 1], P('dp'), may hold values from 0 to 7; in each aligned block of 64 rows (0 to 63, 64 to 127, ...) at most 16 rows name the same one
- prompt_slot: int32 [8], replicated, may hold values from 0 to 7, each once
- suffix_len: int32 [512], P('dp'), may hold values from 32 to 128
Outputs:
- attended: bfloat16 [512, 16384], P('dp', 'tp')
Inputs may be any that keep to these rules, and one draw needn't show every extreme that they name: `fork_prompt`: among the 64 forks of one index of dp no prompt is named more than 16 times. `prompt_slot`: each slot holds exactly one prompt.
All inputs are finite; a program needn't handle non-finite values.
Results may differ from a plain program's by a relative error of at most 0.033.
Values may be sent and summed in bfloat16 or wider, within the bound.
A program may use at most 128 MiB of HBM per device.

v0:
```python
import jax
import jax.numpy as jnp
from jax import lax
from jax.sharding import PartitionSpec as P

R = 512
P_SIZE = 64
V = 128


score_scale = 192.0 ** (-0.5)


def project(latent, w_uv):
    return jnp.einsum("nhr,hrv->nhv", latent, w_uv, preferred_element_type=jnp.float32).astype(
        jnp.bfloat16
    )


def shards(queries, prefix_cache, suffix_cache, w_uv, fork_prompt, prompt_slot, suffix_len):
    owners_count = lax.axis_size("dp")
    forks_here = queries.shape[0]
    heads_here = w_uv.shape[0]
    key_width = R + P_SIZE
    capacity = max(2, 2 * forks_here // owners_count)
    slots_all = owners_count * capacity
    prompt_ids = jnp.arange(prompt_slot.shape[0], dtype=jnp.int32)
    chosen = fork_prompt[:, 0][:, None] == prompt_ids[None, :]
    owner_slot = jnp.sum(jnp.where(chosen, prompt_slot[None, :], 0), axis=1)
    fork_order = jnp.arange(forks_here, dtype=jnp.int32)
    before = (owner_slot[:, None] == owner_slot[None, :]) & (
        fork_order[None, :] < fork_order[:, None]
    )
    slot_rank = jnp.sum(before.astype(jnp.int32), axis=1)
    target = owner_slot * capacity + slot_rank
    placing = target[None, :] == jnp.arange(slots_all, dtype=jnp.int32)[:, None]
    outbound = jnp.dot(
        placing.astype(jnp.bfloat16), queries, preferred_element_type=jnp.float32
    ).astype(jnp.bfloat16)
    outbound = outbound.reshape(owners_count, capacity, heads_here * key_width)
    gathered = lax.all_gather(prefix_cache, "tp", axis=2, tiled=True)[0]
    received = lax.all_to_all(outbound, "dp", split_axis=0, concat_axis=0, tiled=True)
    sources = received.shape[0]
    items = received.shape[1]
    lead_rows = sources * items
    query_rows = received.reshape(lead_rows * heads_here, key_width)
    scores = jnp.dot(query_rows, gathered, preferred_element_type=jnp.float32) * score_scale
    peak_score = jnp.max(scores, axis=1, keepdims=True)
    weights = jnp.exp(scores - peak_score)
    mass_sum = jnp.sum(weights, axis=1)
    summed = lax.dot_general(
        weights.astype(jnp.bfloat16),
        gathered[:R],
        (((1,), (1,)), ((), ())),
        preferred_element_type=jnp.float32,
    )
    latent = (summed / mass_sum[:, None]).astype(jnp.bfloat16)
    log_mass = (peak_score[:, 0] + jnp.log(mass_sum)).reshape(sources, items, heads_here)
    result = project(latent.reshape(lead_rows, heads_here, R), w_uv)
    result = result.reshape(sources, items, heads_here * V)
    answer, answer_mass = (
        lax.all_to_all(result, "dp", split_axis=0, concat_axis=0, tiled=True),
        lax.all_to_all(
            log_mass.astype(jnp.bfloat16), "dp", split_axis=0, concat_axis=0, tiled=True
        ).astype(log_mass.dtype),
    )
    picking = placing.astype(jnp.bfloat16)
    flat_answer = answer.reshape(slots_all, answer.shape[2])
    returned = lax.dot_general(
        picking, flat_answer, (((0,), (0,)), ((), ())), preferred_element_type=jnp.float32
    ).astype(jnp.bfloat16)
    mass_prefix = lax.dot_general(
        placing.astype(jnp.float32),
        answer_mass.reshape(slots_all, heads_here),
        (((0,), (0,)), ((), ())),
        precision=lax.Precision.HIGHEST,
    )
    value_prefix = returned.reshape(forks_here, heads_here, V)
    query_heads = queries.reshape(forks_here, heads_here, key_width)
    suffix_scores = (
        jnp.einsum("fhe,fes->fhs", query_heads, suffix_cache, preferred_element_type=jnp.float32)
        * score_scale
    )
    positions = jnp.arange(suffix_cache.shape[2], dtype=jnp.int32)
    live_mask = (positions[None, :] < suffix_len[:, None])[:, None, :]
    suffix_scores = jnp.where(live_mask, suffix_scores, -jnp.inf)
    suffix_peak = jnp.max(suffix_scores, axis=2, keepdims=True)
    suffix_weights = jnp.where(live_mask, jnp.exp(suffix_scores - suffix_peak), 0.0)
    suffix_sum = jnp.sum(suffix_weights, axis=2)
    suffix_summed = jnp.einsum(
        "fhs,frs->fhr",
        suffix_weights.astype(jnp.bfloat16),
        suffix_cache[:, :R, :],
        preferred_element_type=jnp.float32,
    )
    latent_suffix = (suffix_summed / suffix_sum[..., None]).astype(jnp.bfloat16)
    mass_suffix = suffix_peak[..., 0] + jnp.log(suffix_sum)
    value_suffix = project(latent_suffix, w_uv)
    top_mass = jnp.maximum(mass_prefix, mass_suffix)
    share_prefix = jnp.exp(mass_prefix - top_mass)[..., None]
    share_suffix = jnp.exp(mass_suffix - top_mass)[..., None]
    combined = (
        share_prefix * value_prefix.astype(jnp.float32)
        + share_suffix * value_suffix.astype(jnp.float32)
    ) / (share_prefix + share_suffix)
    return combined.astype(jnp.bfloat16).reshape(forks_here, heads_here * V)


def solution(mesh):
    placed = (
        P("dp", "tp"),
        P("dp", None, "tp"),
        P("dp", None, None),
        P("tp", None, None),
        P("dp", None),
        P(),
        P("dp"),
    )
    return jax.shard_map(
        shards, mesh=mesh, in_specs=placed, out_specs=P("dp", "tp"), check_vma=False
    )
```

profile of v0, /device:TPU:0, one launch (start us, length us, event | category | flops | bytes accessed | tf_op | source)
XLA Modules:
  0.0 223.7 jit_solution(4718613875727864538)
XLA Ops:
  6.5 0.8 select_reduce_fusion
  7.3 0.2 convert_reduce_fusion
  7.5 5.2 %convolution_convert_fusion = bf16[128,18432]{1,0:T(8,128)(2,1)} fusion(bf16[64,18432]{1,0:T(8,128)(2,1)} %param.7, s32[64]{0:T(128)S(1)} %multiply_add_fusion), kind=kOutput, calls=%fused_computation | convolution fusion | flops 304357376 | bytes 7078144 | tf_op jit(solution)/shard_map/dot_general | solution.py:37
  12.7 7.3 %all-to-all-start = ((bf16[8,16,18432]{2,1,0:T(8,128)(2,1)}), bf16[8,16,18432]{2,1,0:T(8,128)(2,1)}, u32[]{:S(2)}, u32[]{:S(2)}) async-start(bf16[8,16,18432]{2,1,0:T(8,128)(2,1)} %bitcast.46), calls=%async_computation | async-start | bytes 9437184 | tf_op jit(solution)/shard_map/all_to_all | solution.py:42
  20.0 0.0 copy-start
  20.0 0.0 all-gather.2.cloned.1.call-start
  20.0 0.7 all-gather.2.cloned.1.call-update
  20.7 4.5 %reshape.71 = bf16[64,32,576]{2,1,0:T(8,128)(2,1)S(1)} reshape(bf16[64,18432]{1,0:T(8,128)(2,1)} %param.7) | data formatting | bytes 4718592 | tf_op jit(solution)/shard_map/reshape | solution.py:79
  25.2 0.0 copy-done
  25.2 0.1 iota_compare_fusion.4
  25.3 99.2 %all-to-all-done = bf16[8,16,18432]{2,1,0:T(8,128)(2,1)} async-done(((bf16[8,16,18432]{2,1,0:T(8,128)(2,1)}), bf16[8,16,18432]{2,1,0:T(8,128)(2,1)}, u32[]{:S(2)}, u32[]{:S(2)}) %all-to-all-start) | async-done | bytes 4718624 | tf_op jit(solution)/shard_map/all_to_all | solution.py:42
  124.5 9.8 %reshape.69 = bf16[4096,576]{1,0:T(8,128)(2,1)} reshape(bf16[8,16,18432]{2,1,0:T(8,128)(2,1)} %all-to-all-done) | data formatting | bytes 9437184 | tf_op jit(solution)/shard_map/reshape | solution.py:46
  134.3 0.0 all-gather.2.cloned.1.call-done
  134.3 12.2 %multiply_reduce_fusion = (f32[4096]{0:T(1024)S(1)}, f32[4096,1024]{0,1:T(8,128)}) fusion(bf16[4096,576]{1,0:T(8,128)(2,1)} %reshape.69, bf16[1,576,1024]{2,1,0:T(8,128)(2,1)} %all-gather.2.cloned.1.call-done), kind=kOutput, calls=%fused_computation.2 | convolution fusion | flops 4840222720 | bytes 22691840 | tf_op jit(solution)/shard_map/dot_general | solution.py:47
  146.6 8.5 %fusion.1 = f32[4096]{0:T(1024)S(1)} fusion(f32[4096,1024]{0,1:T(8,128)} %get-tuple-element.11, f32[4096]{0:T(1024)S(1)} %get-tuple-element.10), kind=kLoop, calls=%fused_computation.4 | loop fusion | flops 12578816 | bytes 16809984 | tf_op jit(solution)/shard_map/reduce_sum | solution.py:50
  155.1 0.1 convert_element_type.59
  155.2 0.7 reshape.77
  155.9 3.6 %all-to-all-start.1 = ((bf16[8,2,256]{2,1,0:T(2,128)(2,1)}), bf16[8,2,256]{2,1,0:T(2,128)(2,1)S(1)}, u32[]{:S(2)}, u32[]{:S(2)}) async-start(bf16[8,2,256]{2,1,0:T(2,128)(2,1)} %reshape.77), calls=%async_computation.1 | async-start | bytes 16384 | tf_op jit(solution)/shard_map/all_to_all | solution.py:63
  159.5 0.0 copy-start.1
  159.6 9.4 %divide_convert_fusion = bf16[4096,512]{1,0:T(8,128)(2,1)S(1)} fusion(f32[4096]{0:T(1024)S(1)} %fusion.1, f32[4096,1024]{0,1:T(8,128)} %get-tuple-element.11, f32[4096]{0:T(1024)S(1)} %get-tuple-element.10, bf16[1,576,1024]{2,1,0:T(8,128)(2,1)} %all-gather.2.cloned.1.call-done), kind=kOutput, calls=%fused_computation.8 | convolution fusion | flops 4311744512 | bytes 22052864 | tf_op jit(solution)/shard_map/dot_general | solution.py:51
  169.0 0.0 copy-done.1
  169.0 4.9 %fusion.18 = bf16[128,32,128]{2,0,1:T(8,128)(2,1)S(1)} fusion(bf16[32,512,128]{2,1,0:T(8,128)(2,1)S(1)} %copy-done.1, bf16[128,32,512]{2,1,0:T(8,128)(2,1)S(1)} %bitcast.49), kind=kOutput, calls=%fused_computation.19 | convolution fusion | flops 537395200 | bytes 9437184 | tf_op jit(solution)/shard_map/nhr,hrv->nhv/dot_general | solution.py:15
  173.8 1.7 copy.26
  175.6 2.3 %reshape.73 = bf16[8,16,4096]{2,1,0:T(8,128)(2,1)} reshape(bf16[128,32,128]{2,1,0:T(8,128)(2,1)} %copy.26) | data formatting | bytes 2097152 | tf_op jit(solution)/shard_map/reshape | solution.py:60
  177.9 0.0 all-to-all-done.1
  177.9 6.0 %all-to-all-start.2 = ((bf16[8,16,4096]{2,1,0:T(8,128)(2,1)}), bf16[8,16,4096]{2,1,0:T(8,128)(2,1)}, u32[]{:S(2)}, u32[]{:S(2)}) async-start(bf16[8,16,4096]{2,1,0:T(8,128)(2,1)} %reshape.73), calls=%async_computation.2 | async-start | bytes 2097152 | tf_op jit(solution)/shard_map/all_to_all | solution.py:62
  183.8 6.3 %fusion.69 = (f32[64,32]{1,0:T(8,128)S(1)}, f32[64,32,128]{2,1,0:T(8,128)}) fusion(bf16[64,32,576]{2,1,0:T(8,128)(2,1)S(1)} %reshape.71, bf16[64,576,128]{2,1,0:T(8,128)(2,1)} %param.9, pred[64,128]{1,0:T(8,128)(4,1)S(1)} %iota_compare_fusion.4), kind=kOutput, calls=%fused_computation.63 | convolution fusion | flops 302774272 | bytes 12861440 | tf_op jit(solution)/shard_map/fhe,fes->fhs/dot_general | solution.py:81
  190.1 0.1 copy.24
  190.2 1.9 fusion.52
  192.1 0.1 copy.23
  192.1 6.7 %divide_convert_fusion.1 = bf16[64,32,512]{2,1,0:T(8,128)(2,1)S(1)} fusion(f32[64,32]{1,0:T(8,128)S(1)} %fusion.52, bf16[64,576,128]{2,1,0:T(8,128)(2,1)} %param.9, f32[64,32,128]{2,1,0:T(8,128)} %get-tuple-element.9, f32[64,32]{1,0:T(8,128)S(1)} %get-tuple-element.8, pred[64,128]{1,0:T(8,128)(4,1)S(1)} %iota_compare_fusion.4), kind=kOutput, calls=%fused_computation.15 | convolution fusion | flops 271319040 | bytes 11558912 | tf_op jit(solution)/shard_map/fhs,frs->fhr/dot_general | solution.py:90
  198.9 0.1 reshape.78
  199.0 0.2 fusion.66
  199.2 10.3 %all-to-all-done.2 = bf16[8,16,4096]{2,1,0:T(8,128)(2,1)} async-done(((bf16[8,16,4096]{2,1,0:T(8,128)(2,1)}), bf16[8,16,4096]{2,1,0:T(8,128)(2,1)}, u32[]{:S(2)}, u32[]{:S(2)}) %all-to-all-start.2) | async-done | bytes 1048608 | tf_op jit(solution)/shard_map/all_to_all | solution.py:62
  209.5 1.6 fusion.21
  211.1 4.8 %fusion.48 = bf16[32,8,8,128]{3,2,1,0:T(8,128)(2,1)S(1)} fusion(bf16[32,512,128]{2,1,0:T(8,128)(2,1)} %param.10, bf16[64,32,512]{2,1,0:T(8,128)(2,1)S(1)} %divide_convert_fusion.1, f32[8,32,8,128]{3,2,1,0:T(8,128)S(1)} %fusion.21, f32[64,32]{0,1:T(8,128)S(1)} %get-tuple-element.5, f32[64,32]{0,1:T(8,128)S(1)} %get-tuple-element.6, ...), kind=kOutput, calls=%fused_computation.32 | convolution fusion | flops 270270464 | bytes 7888896 | tf_op jit(solution)/shard_map/nhr,hrv->nhv/dot_general | solution.py:15
  215.9 0.9 copy.58
  (2 shorter events, 0.0 us)
Async XLA Ops:
  12.7 111.8 %all-to-all-start = ((bf16[8,16,18432]{2,1,0:T(8,128)(2,1)}), bf16[8,16,18432]{2,1,0:T(8,128)(2,1)}, u32[]{:S(2)}, u32[]{:S(2)}) async-start(bf16[8,16,18432]{2,1,0:T(8,128)(2,1)} %bitcast.46), calls=%async_computation | async-start | bytes 9437184 | tf_op jit(solution)/shard_map/all_to_all | solution.py:42
  20.0 5.2 %copy-start = (s32[64]{0:T(128)S(1)}, s32[64]{0:T(128)}, u32[]{:S(2)}) copy-start(s32[64]{0:T(128)} %param.13) | copy-start | bytes 772
  20.0 114.4 %all-gather.2.cloned.1.call-start = ((), (), s32[]{:S(2)}) async-start(), calls=%async_computation.3 | async-start | bytes 1474560 | tf_op jit(solution)/shard_map/all_gather | solution.py:41
  155.9 22.0 %all-to-all-start.1 = ((bf16[8,2,256]{2,1,0:T(2,128)(2,1)}), bf16[8,2,256]{2,1,0:T(2,128)(2,1)S(1)}, u32[]{:S(2)}, u32[]{:S(2)}) async-start(bf16[8,2,256]{2,1,0:T(2,128)(2,1)} %reshape.77), calls=%async_computation.1 | async-start | bytes 16384 | tf_op jit(solution)/shard_map/all_to_all | solution.py:63
  159.5 9.4 %copy-start.1 = (bf16[32,512,128]{2,1,0:T(8,128)(2,1)S(1)}, bf16[32,512,128]{2,1,0:T(8,128)(2,1)}, u32[]{:S(2)}) copy-start(bf16[32,512,128]{2,1,0:T(8,128)(2,1)} %param.10) | copy-start | bytes 12582916
  177.9 31.6 %all-to-all-start.2 = ((bf16[8,16,4096]{2,1,0:T(8,128)(2,1)}), bf16[8,16,4096]{2,1,0:T(8,128)(2,1)}, u32[]{:S(2)}, u32[]{:S(2)}) async-start(bf16[8,16,4096]{2,1,0:T(8,128)(2,1)} %reshape.73), calls=%async_computation.2 | async-start | bytes 2097152 | tf_op jit(solution)/shard_map/all_to_all | solution.py:62
Sparse Core Ops, SparseCore 0:
  22.3 18.9 all-gather.1
where the time goes:
time: 224 us
  waiting for transfers between devices  110 us (49%)
  matrix products  51.4 us (23%)
  local copies, waits for them, and re-layouts  20.3 us (9%)
  starting transfers between devices  16.9 us (8%)
  between operations  13.5 us (6%)
  other arithmetic  11.4 us (5%)
    all_to_all x1, waiting for transfers between devices, shards(): lax.all_to_all(outbound, 'dp', split_axis=0, concat_axis=0, tiled=True)  99.2 us
    dot_general x1, matrix products, shards(): jnp.dot(query_rows, gathered, preferred_element_type=jnp.float32)  12.2 us
    all_to_all x1, waiting for transfers between devices, shards(): lax.all_to_all(result, 'dp', split_axis=0, concat_axis=0, tiled=True)  10.3 us
    reshape x1, local copies, waits for them, and re-layouts, shards(): query_rows = received.reshape(lead_rows * heads_here, key_width)  9.84 us
    dot_general x2, matrix products, project(): jnp.einsum('nhr,hrv->nhv', latent, w_uv, preferred_element_type=jnp.float32)  9.7 us
    dot_general x1, matrix products, shards(): lax.dot_general(weights.astype(jnp.bfloat16), gathered[:R], (((1,), (1,))...  9.4 us
    reduce_sum x1, other arithmetic, shards(): mass_sum = jnp.sum(weights, axis=1)  8.53 us
    all_to_all x1, starting transfers between devices, shards(): lax.all_to_all(outbound, 'dp', split_axis=0, concat_axis=0, tiled=True)  7.28 us
  transfers between devices with their start and end apart: 4, of which 2 were waited for; matrix products, arithmetic and copies ran while one was open for 21% of the time, Pallas kernels for 0%

commit v1 on v0

--- a/solution.py
+++ b/solution.py
@@ -1,6 +1,10 @@
+import functools
+
 import jax
 import jax.numpy as jnp
 from jax import lax
+from jax.experimental import pallas as pl
+from jax.experimental.pallas import tpu as pltpu
 from jax.sharding import PartitionSpec as P
 
 R = 512
@@ -9,6 +13,8 @@
 
 
 score_scale = 192.0 ** (-0.5)
+log2e = 1.4426950408889634
+OUTER = (((1,), (1,)), ((), ()))
 
 
 def project(latent, w_uv):
@@ -17,7 +23,7 @@
     )
 
 
-def shards(queries, prefix_cache, suffix_cache, w_uv, fork_prompt, prompt_slot, suffix_len):
+def exchange_plan(queries, prefix_cache, suffix_cache, w_uv, fork_prompt, prompt_slot, suffix_len):
     owners_count = lax.axis_size("dp")
     forks_here = queries.shape[0]
     heads_here = w_uv.shape[0]
@@ -106,6 +112,170 @@
     return combined.astype(jnp.bfloat16).reshape(forks_here, heads_here * V)
 
 
+def suffix_kernel(lens_ref, q_ref, cache_ref, latent_ref, mass_ref):
+    block = q_ref.shape[0]
+    first = pl.program_id(0) * block
+    positions = lax.broadcasted_iota(jnp.int32, (1, cache_ref.shape[2]), 1)
+    for i in range(block):
+        live = positions < lens_ref[first + i]
+        scores = jnp.dot(q_ref[i], cache_ref[i], preferred_element_type=jnp.float32)
+        scores = jnp.where(live, scores * score_scale, -jnp.inf)
+        peak = jnp.max(scores, axis=1, keepdims=True)
+        weights = jnp.exp(scores - peak)
+        mass = jnp.sum(weights, axis=1, keepdims=True)
+        summed = lax.dot_general(
+            weights.astype(jnp.bfloat16),
+            cache_ref[i, :R, :],
+            OUTER,
+            preferred_element_type=jnp.float32,
+        )
+        latent_ref[i] = (summed / mass).astype(jnp.bfloat16)
+        mass_ref[i] = jnp.broadcast_to(peak + jnp.log(mass), mass_ref.shape[1:])
+
+
+def suffix_attention(query_heads, suffix_cache, suffix_len, block=8):
+    forks, heads, width = query_heads.shape
+    keys = suffix_cache.shape[2]
+    return pl.pallas_call(
+        suffix_kernel,
+        grid_spec=pltpu.PrefetchScalarGridSpec(
+            num_scalar_prefetch=1,
+            grid=(forks // block,),
+            in_specs=[
+                pl.BlockSpec((block, heads, width), lambda i, lens: (i, 0, 0)),
+                pl.BlockSpec((block, width, keys), lambda i, lens: (i, 0, 0)),
+            ],
+            out_specs=[
+                pl.BlockSpec((block, heads, R), lambda i, lens: (i, 0, 0)),
+                pl.BlockSpec((block, heads, 128), lambda i, lens: (i, 0, 0)),
+            ],
+        ),
+        out_shape=[
+            jax.ShapeDtypeStruct((forks, heads, R), jnp.bfloat16),
+            jax.ShapeDtypeStruct((forks, heads, 128), jnp.float32),
+        ],
+        cost_estimate=pl.CostEstimate(
+            flops=16 * forks * heads * keys * (width + R),
+            bytes_accessed=2 * suffix_cache.size + 2 * query_heads.size,
+            transcendentals=forks * heads * keys,
+        ),
+        name="suffix",
+    )(suffix_len, query_heads, suffix_cache)
+
+
+def prefix_kernel(
+    group, starts_ref, order_ref, q_ref, cache_ref, latent_ref, mass_ref, out_ref
+):
+    slot = pl.program_id(0)
+    heads = q_ref.shape[1]
+    first = starts_ref[slot]
+    last = starts_ref[slot + 1] - 1
+    parts = cache_ref.shape[1]
+
+    def one_group(g, carry):
+        ids = [order_ref[jnp.minimum(first + g * group + i, last)] for i in range(group)]
+        rows = jnp.concatenate([q_ref[fork] for fork in ids], axis=0)
+        scores = [
+            jnp.dot(rows, cache_ref[0, k], preferred_element_type=jnp.float32)
+            for k in range(parts)
+        ]
+        peak = functools.reduce(
+            jnp.maximum, [jnp.max(piece, axis=1, keepdims=True) for piece in scores]
+        )
+        mass = 0.0
+        summed = 0.0
+        for k in range(parts):
+            weights = jnp.exp2((scores[k] - peak) * (score_scale * log2e))
+            mass = mass + jnp.sum(weights, axis=1, keepdims=True)
+            summed = summed + lax.dot_general(
+                weights.astype(jnp.bfloat16),
+                cache_ref[0, k, :R, :],
+                OUTER,
+                preferred_element_type=jnp.float32,
+            )
+        peak = peak * score_scale
+        for i, fork in enumerate(ids):
+            own = slice(i * heads, (i + 1) * heads)
+            other = mass_ref[fork][:, :1]
+            top = jnp.maximum(peak[own], other)
+            ours = jnp.exp(peak[own] - top)
+            theirs = jnp.exp(other - top)
+            share = 1.0 / (ours * mass[own] + theirs)
+            out_ref[fork] = (
+                summed[own] * (ours * share)
+                + latent_ref[fork].astype(jnp.float32) * (theirs * share)
+            ).astype(jnp.bfloat16)
+        return carry
+
+    lax.fori_loop(0, (last - first + group) // group, one_group, 0)
+
+
+def prefix_attention(starts, order, query_heads, caches, latent_suffix, mass_suffix, group=8):
+    forks, heads, width = query_heads.shape
+    slots, parts, _, keys = caches.shape
+    whole = lambda s, a, b: (0, 0, 0)
+    return pl.pallas_call(
+        functools.partial(prefix_kernel, group),
+        grid_spec=pltpu.PrefetchScalarGridSpec(
+            num_scalar_prefetch=2,
+            grid=(slots,),
+            in_specs=[
+                pl.BlockSpec((forks, heads, width), whole),
+                pl.BlockSpec((1, parts, width, keys), lambda s, a, b: (s, 0, 0, 0)),
+                pl.BlockSpec((forks, heads, R), whole),
+                pl.BlockSpec((forks, heads, 128), whole),
+            ],
+            out_specs=pl.BlockSpec((forks, heads, R), whole),
+        ),
+        out_shape=jax.ShapeDtypeStruct((forks, heads, R), jnp.bfloat16),
+        cost_estimate=pl.CostEstimate(
+            flops=2 * forks * heads * parts * keys * (width + R),
+            bytes_accessed=2 * caches.size + 2 * query_heads.size,
+            transcendentals=forks * heads * parts * keys,
+        ),
+        compiler_params=pltpu.CompilerParams(vmem_limit_bytes=48 * 1024 * 1024),
+        name="prefix",
+    )(starts, order, query_heads, caches, latent_suffix, mass_suffix)
+
+
+def fork_order(fork_prompt, prompt_slot):
+    forks = fork_prompt.shape[0]
+    prompt_ids = jnp.arange(prompt_slot.shape[0], dtype=jnp.int32)
+    chosen = fork_prompt[:, 0][:, None] == prompt_ids[None, :]
+    owner_slot = jnp.sum(jnp.where(chosen, prompt_slot[None, :], 0), axis=1)
+    ids = jnp.arange(forks, dtype=jnp.int32)
+    key = owner_slot * forks + ids
+    place = jnp.sum((key[None, :] < key[:, None]).astype(jnp.int32), axis=1)
+    order = jnp.sum(jnp.where(place[None, :] == ids[:, None], ids[None, :], 0), axis=1)
+    edges = jnp.arange(prompt_slot.shape[0] + 1, dtype=jnp.int32)
+    starts = jnp.sum((owner_slot[None, :] < edges[:, None]).astype(jnp.int32), axis=1)
+    return starts, order
+
+
+def gather_plan(queries, prefix_cache, suffix_cache, w_uv, fork_prompt, prompt_slot, suffix_len):
+    forks_here = queries.shape[0]
+    heads_here = w_uv.shape[0]
+    owners_count = lax.axis_size("dp")
+    tp_count = lax.axis_size("tp")
+    caches = lax.all_gather(prefix_cache[0], ("dp", "tp"), axis=0)
+    caches = caches.reshape(owners_count, tp_count, *prefix_cache.shape[1:])
+    starts, order = fork_order(fork_prompt, prompt_slot)
+    query_heads = queries.reshape(forks_here, heads_here, R + P_SIZE)
+    latent_suffix, mass_suffix = suffix_attention(query_heads, suffix_cache, suffix_len)
+    latent = prefix_attention(starts, order, query_heads, caches, latent_suffix, mass_suffix)
+    return project(latent, w_uv).reshape(forks_here, heads_here * V)
+
+
+def shards(queries, prefix_cache, *others):
+    owners_count = lax.axis_size("dp")
+    forks_here = queries.shape[0]
+    capacity = max(2, 2 * forks_here // owners_count)
+    sent = owners_count * capacity * queries.shape[1]
+    gathered = owners_count * lax.axis_size("tp") * prefix_cache.size
+    plan = gather_plan if gathered <= 4 * sent else exchange_plan
+    return plan(queries, prefix_cache, *others)
+
+
 def solution(mesh):
     placed = (
         P("dp", "tp"),

time: 224 us -> 123 us (0.55)
  matrix products: 51.4 us -> 2.52 us
  waiting for transfers between devices: 110 us -> 62.8 us
  Pallas kernels: 0 us -> 34.1 us
  starting transfers between devices: 16.9 us -> 0.01 us
  local copies, waits for them, and re-layouts: 20.3 us -> 9.3 us
  other arithmetic: 11.4 us -> 0.5 us
    all_to_all x3 -> x0, waiting for transfers between devices: 110 us -> none  [the longest x1 99.2 us: shards(): lax.all_to_all(outbound, 'dp', split_axis=0, concat_axis=0, tiled=True)]
    all_gather x1, waiting for transfers between devices: 0.01 us -> 62.1 us  [gather_plan(): caches = lax.all_gather(prefix_cache[0], ('dp', 'tp'), axis=0)]
    dot_general x7 -> x0, matrix products: 41.7 us -> none  [the longest x1 12.2 us: shards(): jnp.dot(query_rows, gathered, preferred_element_type=jnp.float32)]
    pallas_call x0 -> x2, Pallas kernels: none -> 34.1 us  [the longest x1 19 us: suffix_attention(): pl.pallas_call(suffix_kernel, grid_spec=pltpu.PrefetchScalarGridSpec(num_...]
    all_to_all x3 -> x0, starting transfers between devices: 16.9 us -> none  [the longest x1 7.28 us: shards(): lax.all_to_all(outbound, 'dp', split_axis=0, concat_axis=0, tiled=True)]
    reshape x4 -> x2, local copies, waits for them, and re-layouts: 17.5 us -> 6.47 us  [the longest x1 5.58 us: gather_plan(): query_heads = queries.reshape(forks_here, heads_here, R + P_SIZE)]
    reduce_sum x4, other arithmetic: 11.3 us -> 0.49 us  [the longest x1 0.17 us: fork_order(): place = jnp.sum((key[None, :] < key[:, None]).astype(jnp.int32), axis=1)]
    dot_general x2 -> x1, matrix products: 9.7 us -> 2.52 us  [project(): jnp.einsum('nhr,hrv->nhv', latent, w_uv, preferred_element_type=jnp.float32)]
  transfers between devices with their start and end apart: 4 -> 1, of which waited for: 2 -> 1; matrix products, arithmetic and copies ran while one was open for 21% -> 5% of each run, Pallas kernels for 0% -> 16%
where the time goes in v1:
time: 123 us
  waiting for transfers between devices  62.8 us (51%)
  Pallas kernels  34.1 us (28%)
  between operations  13.4 us (11%)
  local copies, waits for them, and re-layouts  9.3 us (8%)
  matrix products  2.52 us (2%)
    all_gather x1, waiting for transfers between devices, gather_plan(): caches = lax.all_gather(prefix_cache[0], ('dp', 'tp'), axis=0)  62.1 us
    pallas_call x1, Pallas kernels, suffix_attention(): pl.pallas_call(suffix_kernel, grid_spec=pltpu.PrefetchScalarGridSpec(num_...  19 us
    pallas_call x1, Pallas kernels, prefix_attention(): pl.pallas_call(functools.partial(prefix_kernel, group), grid_spec=pltpu.P...  15.1 us
    reshape x1, local copies, waits for them, and re-layouts, gather_plan(): query_heads = queries.reshape(forks_here, heads_here, R + P_SIZE)  5.58 us
    unnamed x10, local copies, waits for them, and re-layouts  2.83 us
    dot_general x1, matrix products, project(): jnp.einsum('nhr,hrv->nhv', latent, w_uv, preferred_element_type=jnp.float32)  2.52 us
  transfers between devices with their start and end apart: 1, of which 1 were waited for; matrix products, arithmetic and copies ran while one was open for 5% of the time, Pallas kernels for 16%

profile of v1, /device:TPU:0, one launch (start us, length us, event | category | flops | bytes accessed | tf_op | source)
XLA Modules:
  0.0 122.6 jit_solution(6923717668072490846)
XLA Ops:
  6.5 0.0 copy-start.3
  6.5 0.0 copy-start.4
  6.5 0.0 all-gather.2.cloned.1.call-start
  6.5 0.7 all-gather.2.cloned.1.call-update
  7.3 5.6 %reshape.26.q_ref = bf16[64,32,576]{2,1,0:T(8,128)(2,1)} reshape(bf16[64,18432]{1,0:T(8,128)(2,1)} %param.7) | data formatting | bytes 4718592 | tf_op jit(solution)/shard_map/reshape | solution.py:263
  12.8 0.0 copy-done.3
  12.8 0.0 copy-done.4
  12.8 0.1 select_reduce_fusion.1
  12.9 0.1 convert_reduce_fusion.1.starts_ref
  13.1 0.2 convert_reduce_fusion
  13.2 0.1 select_reduce_fusion.order_ref
  13.3 19.0 %suffix.1 = (bf16[64,32,512]{2,1,0:T(8,128)(2,1)}, f32[64,32,128]{2,1,0:T(8,128)}) custom-call(s32[64]{0:T(128)} %lens_ref.1, bf16[64,32,576]{2,1,0:T(8,128)(2,1)} %reshape.26.q_ref, bf16[64,576,128]{2,1,0:T(8,128)(2,1)} %cache_ref.1), custom_call_target="tpu_custom_call" | custom-call | flops 4563402752 | bytes 11796480 | tf_op jit(solution)/shard_map/suffix/pallas_call | solution.py:139
  32.4 62.1 %all-gather.2.cloned.1.call-done = bf16[32,576,256]{2,1,0:T(8,128)(2,1)} async-done(((bf16[1,576,256]{2,1,0:T(8,128)(2,1)}), bf16[32,576,256]{2,1,0:T(8,128)(2,1)}) %all-gather.2.cloned.1.call-update) | async-done | bytes 9437200 | tf_op jit(solution)/shard_map/all_gather | solution.py:260
  94.4 0.0 copy-start
  94.4 1.6 %copy-done = bf16[64,32,512]{2,1,0:T(8,128)(2,1)S(1)} copy-done((bf16[64,32,512]{2,1,0:T(8,128)(2,1)S(1)}, bf16[64,32,512]{2,1,0:T(8,128)(2,1)}, u32[]{:S(2)}) %copy-start) | copy-done | bytes 2097176
  96.0 0.0 copy-start.1
  96.0 1.2 copy-done.1
  97.3 0.0 copy-start.2
  97.3 15.1 %prefix.1 = bf16[64,32,512]{2,1,0:T(8,128)(2,1)S(1)} custom-call(s32[9]{0:T(128)S(1)} %convert_reduce_fusion.1.starts_ref, s32[64]{0:T(128)S(1)} %select_reduce_fusion.order_ref, bf16[64,32,576]{2,1,0:T(8,128)(2,1)} %reshape.26.q_ref, bf16[8,4,576,256]{3,2,1,0:T(8,128)(2,1)} %bitcast.9, bf16[64,32,512]{2,1,0:T(8,128)(2,1)S(1)} %copy-done, ...), custom_call_target="tpu_custom_call" | custom-call | flops 4563402752 | bytes 11796480 | tf_op jit(solution)/shard_map/prefix/pallas_call | solution.py:217
  112.4 0.0 copy-done.2
  112.4 2.5 %fusion.5 = bf16[32,8,8,128]{3,2,1,0:T(8,128)(2,1)S(1)} fusion(bf16[32,512,128]{2,1,0:T(8,128)(2,1)S(1)} %copy-done.2, bf16[64,32,512]{2,1,0:T(8,128)(2,1)S(1)} %prefix.1), kind=kOutput, calls=%fused_computation.3 | convolution fusion | flops 268697600 | bytes 6815744 | tf_op jit(solution)/shard_map/nhr,hrv->nhv/dot_general | solution.py:21
  114.9 0.9 copy.23
  (1 shorter events, 0.0 us)
Async XLA Ops:
  6.5 6.3 %copy-start.3 = (s32[8]{0:T(128)S(1)}, s32[8]{0:T(128)}, u32[]{:S(2)}) copy-start(s32[8]{0:T(128)} %param.12) | copy-start | bytes 100
  6.5 6.3 %copy-start.4 = (s32[64,1]{0,1:T(1,128)S(1)}, s32[64,1]{0,1:T(1,128)}, u32[]{:S(2)}) copy-start(s32[64,1]{0,1:T(1,128)} %param.11) | copy-start | bytes 772
  6.5 87.9 %all-gather.2.cloned.1.call-start = ((), (), s32[]{:S(2)}) async-start(), calls=%async_computation | async-start | bytes 9732096 | tf_op jit(solution)/shard_map/all_gather | solution.py:260
  94.4 1.6 %copy-start = (bf16[64,32,512]{2,1,0:T(8,128)(2,1)S(1)}, bf16[64,32,512]{2,1,0:T(8,128)(2,1)}, u32[]{:S(2)}) copy-start(bf16[64,32,512]{2,1,0:T(8,128)(2,1)} %get-tuple-element.7.latent_ref) | copy-start | bytes 6291460
  96.0 1.2 copy-start.1
  97.3 15.1 %copy-start.2 = (bf16[32,512,128]{2,1,0:T(8,128)(2,1)S(1)}, bf16[32,512,128]{2,1,0:T(8,128)(2,1)}, u32[]{:S(2)}) copy-start(bf16[32,512,128]{2,1,0:T(8,128)(2,1)} %param.10) | copy-start | bytes 12582916
Sparse Core Ops, SparseCore 0:
  10.2 84.1 all-gather.1

commit v2 on v1

--- a/solution.py
+++ b/solution.py
@@ -112,55 +112,266 @@
     return combined.astype(jnp.bfloat16).reshape(forks_here, heads_here * V)
 
 
-def suffix_kernel(lens_ref, q_ref, cache_ref, latent_ref, mass_ref):
-    block = q_ref.shape[0]
-    first = pl.program_id(0) * block
+MESH = pl.DeviceIdType.MESH
+
+
+def suffix_fork(i, lens_ref, q_ref, cache_ref, latent_ref, mass_ref):
     positions = lax.broadcasted_iota(jnp.int32, (1, cache_ref.shape[2]), 1)
-    for i in range(block):
-        live = positions < lens_ref[first + i]
-        scores = jnp.dot(q_ref[i], cache_ref[i], preferred_element_type=jnp.float32)
-        scores = jnp.where(live, scores * score_scale, -jnp.inf)
-        peak = jnp.max(scores, axis=1, keepdims=True)
-        weights = jnp.exp(scores - peak)
-        mass = jnp.sum(weights, axis=1, keepdims=True)
-        summed = lax.dot_general(
-            weights.astype(jnp.bfloat16),
-            cache_ref[i, :R, :],
-            OUTER,
-            preferred_element_type=jnp.float32,
+    live = positions < lens_ref[i]
+    scores = jnp.dot(q_ref[i], cache_ref[i], preferred_element_type=jnp.float32)
+    scores = jnp.where(live, scores * score_scale, -jnp.inf)
+    peak = jnp.max(scores, axis=1, keepdims=True)
+    weights = jnp.exp(scores - peak)
+    mass = jnp.sum(weights, axis=1, keepdims=True)
+    summed = lax.dot_general(
+        weights.astype(jnp.bfloat16),
+        cache_ref[i, :R, :],
+        OUTER,
+        preferred_element_type=jnp.float32,
+    )
+    latent_ref[i] = (summed / mass).astype(jnp.bfloat16)
+    mass_ref[i] = jnp.broadcast_to(peak + jnp.log(mass), mass_ref.shape[1:])
+
+
+def gather_kernel(
+    planes,
+    steps,
+    lens_ref,
+    own_ref,
+    q_ref,
+    suffix_ref,
+    out_ref,
+    latent_ref,
+    mass_ref,
+    held,
+    load_sem,
+    own_sem,
+    z_send,
+    z_recv,
+    x_send,
+    x_recv,
+    y_send,
+    y_recv,
+    dx_send,
+    dx_recv,
+    dy_send,
+    dy_recv,
+    pair_send,
+    pair_recv,
+):
+    dp, tp = lax.axis_index("dp"), lax.axis_index("tp")
+    z, x = dp // 2, dp % 2
+    y, c = tp // 2, tp % 2
+    forks = q_ref.shape[0]
+    block = forks // steps
+    half = own_ref.shape[1] // 2
+    at_x = (z * 2 + (1 - x), tp)
+    at_y = (dp, (1 - y) * 2 + c)
+    at_pair = (dp, y * 2 + (1 - c))
+    at_up = (jnp.minimum(z + 1, planes - 1) * 2 + x, tp)
+    at_down = (jnp.maximum(z - 1, 0) * 2 + x, tp)
+    has_up, has_down = z + 1 < planes, z > 0
+
+    def place(zz, xx, yy):
+        return out_ref.at[zz * 2 + xx, yy * 2 + c]
+
+    def top(ref):
+        return ref.at[pl.ds(0, half)]
+
+    def bottom(ref):
+        return ref.at[pl.ds(half, half)]
+
+    def copy(src, dst, send, recv, device):
+        return pltpu.make_async_remote_copy(
+            src_ref=src,
+            dst_ref=dst,
+            send_sem=send,
+            recv_sem=recv,
+            device_id=device,
+            device_id_type=MESH,
         )
-        latent_ref[i] = (summed / mass).astype(jnp.bfloat16)
-        mass_ref[i] = jnp.broadcast_to(peak + jnp.log(mass), mass_ref.shape[1:])
-
-
-def suffix_attention(query_heads, suffix_cache, suffix_len, block=8):
+
+    def z_copy(zz, device, src=None):
+        to = place(zz, x, y)
+        return copy(to if src is None else src, to, z_send.at[zz], z_recv.at[zz], device)
+
+    def own_up(device, src):
+        to = place(z, x, y)
+        return copy(src, to, z_send.at[planes], z_recv.at[z], device)
+
+    def x_copy(zz, src=None):
+        to = place(zz, x, y)
+        return copy(to if src is None else src, to, x_send.at[zz], x_recv.at[zz], at_x)
+
+    def y_copy(zz, src=None):
+        to = place(zz, x, y)
+        return copy(to if src is None else src, to, y_send.at[zz], y_recv.at[zz], at_y)
+
+    def dy_copy(zz):
+        part = top(place(zz, 1 - x, y))
+        return copy(part, part, dy_send.at[zz], dy_recv.at[zz], at_y)
+
+    def dx_copy(zz):
+        part = bottom(place(zz, x, 1 - y))
+        return copy(part, part, dx_send.at[zz], dx_recv.at[zz], at_x)
+
+    def pair_copy(zz, xx, yy, src=None):
+        to = place(zz, xx, yy)
+        k = (zz * 2 + xx) * 2 + yy
+        src = to if src is None else src
+        return copy(src, to, pair_send.at[k], pair_recv.at[k], at_pair)
+
+    def load(s):
+        part = pl.ds(s * block, block)
+        return pltpu.make_async_copy(suffix_ref.at[part], held.at[part], load_sem.at[s])
+
+    for s in range(steps):
+        load(s).start()
+
+    barrier = pltpu.get_barrier_semaphore()
+    for device in (at_x, at_y, at_pair):
+        pl.semaphore_signal(barrier, inc=1, device_id=device, device_id_type=MESH)
+
+    @pl.when(has_up)
+    def _():
+        pl.semaphore_signal(barrier, inc=1, device_id=at_up, device_id_type=MESH)
+
+    @pl.when(has_down)
+    def _():
+        pl.semaphore_signal(barrier, inc=1, device_id=at_down, device_id_type=MESH)
+
+    pl.semaphore_wait(barrier, 3 + has_up.astype(jnp.int32) + has_down.astype(jnp.int32))
+
+    mine = own_ref.at[0]
+
+    @pl.when(has_up)
+    def _():
+        z_copy(z, at_up, mine).start()
+
+    @pl.when(has_down)
+    def _():
+        own_up(at_down, mine).start()
+
+    x_copy(z, mine).start()
+    y_copy(z, mine).start()
+    pair_copy(z, x, y, mine).start()
+    local = pltpu.make_async_copy(mine, place(z, x, y), own_sem)
+    local.start()
+
+    def compute(low, high):
+        def step(s, carry):
+            load(s).wait()
+            for i in range(block):
+                suffix_fork(s * block + i, lens_ref, q_ref, held, latent_ref, mass_ref)
+            return carry
+
+        lax.fori_loop(low, high, step, 0)
+
+    def arrived(d):
+        for sign in (-1, 1):
+            zz = z + sign * d
+            onward = has_up if sign < 0 else has_down
+            device = at_up if sign < 0 else at_down
+
+            @pl.when((zz >= 0) & (zz < planes))
+            def _():
+                z_copy(zz, device).wait_recv()
+
+                @pl.when(onward)
+                def _():
+                    z_copy(zz, device).start()
+
+                x_copy(zz).start()
+                y_copy(zz).start()
+                pair_copy(zz, x, y).start()
+
+    def each(d, act):
+        if d == 0:
+            act(z)
+            return
+        for sign in (-1, 1):
+            zz = z + sign * d
+            pl.when((zz >= 0) & (zz < planes))(functools.partial(act, zz))
+
+    def across(zz):
+        x_copy(zz).wait_recv()
+        dy_copy(zz).start()
+        pair_copy(zz, 1 - x, y).start()
+        y_copy(zz).wait_recv()
+        dx_copy(zz).start()
+        pair_copy(zz, x, 1 - y).start()
+
+    def diagonal(zz):
+        dy_copy(zz).wait_recv()
+        dx_copy(zz).wait_recv()
+        pair_copy(zz, 1 - x, 1 - y).start()
+
+    marks = [steps * r // planes for r in range(planes + 1)]
+    for r in range(planes):
+        if r > 0:
+            arrived(r)
+            each(r - 1, across)
+        if r > 1:
+            each(r - 2, diagonal)
+        compute(marks[r], marks[r + 1])
+    each(planes - 1, across)
+    if planes > 1:
+        each(planes - 2, diagonal)
+    each(planes - 1, diagonal)
+
+    local.wait()
+
+    @pl.when(has_down)
+    def _():
+        own_up(at_down, mine).wait_send()
+
+    for zz in range(planes):
+        sent = ((zz <= z) & has_up) | ((zz > z) & has_down)
+
+        @pl.when(sent)
+        def _():
+            z_copy(zz, at_up).wait_send()
+
+        x_copy(zz).wait_send()
+        y_copy(zz).wait_send()
+        dx_copy(zz).wait_send()
+        dy_copy(zz).wait_send()
+        for xx in range(2):
+            for yy in range(2):
+                pair_copy(zz, xx, yy).wait()
+
+
+def gather_and_suffix(prefix_cache, query_heads, suffix_cache, suffix_len, steps=8):
     forks, heads, width = query_heads.shape
     keys = suffix_cache.shape[2]
+    slots, parts = lax.axis_size("dp"), lax.axis_size("tp")
+    planes = slots // 2
+    dma = pltpu.SemaphoreType.DMA
+    vmem = pl.BlockSpec(memory_space=pltpu.VMEM)
+    hbm = pl.BlockSpec(memory_space=pl.ANY)
     return pl.pallas_call(
-        suffix_kernel,
-        grid_spec=pltpu.PrefetchScalarGridSpec(
-            num_scalar_prefetch=1,
-            grid=(forks // block,),
-            in_specs=[
-                pl.BlockSpec((block, heads, width), lambda i, lens: (i, 0, 0)),
-                pl.BlockSpec((block, width, keys), lambda i, lens: (i, 0, 0)),
-            ],
-            out_specs=[
-                pl.BlockSpec((block, heads, R), lambda i, lens: (i, 0, 0)),
-                pl.BlockSpec((block, heads, 128), lambda i, lens: (i, 0, 0)),
-            ],
-        ),
+        functools.partial(gather_kernel, planes, steps),
+        in_specs=[pl.BlockSpec(memory_space=pltpu.SMEM), hbm, vmem, hbm],
+        out_specs=[hbm, vmem, vmem],
         out_shape=[
+            jax.ShapeDtypeStruct((slots, parts, *prefix_cache.shape[1:]), jnp.bfloat16),
             jax.ShapeDtypeStruct((forks, heads, R), jnp.bfloat16),
             jax.ShapeDtypeStruct((forks, heads, 128), jnp.float32),
         ],
-        cost_estimate=pl.CostEstimate(
-            flops=16 * forks * heads * keys * (width + R),
-            bytes_accessed=2 * suffix_cache.size + 2 * query_heads.size,
-            transcendentals=forks * heads * keys,
+        scratch_shapes=[
+            pltpu.VMEM(suffix_cache.shape, jnp.bfloat16),
+            dma((steps,)),
+            dma,
+            dma((planes + 1,)),
+            *[dma((planes,)) for _ in range(9)],
+            dma((slots * 2,)),
+            dma((slots * 2,)),
+        ],
+        compiler_params=pltpu.CompilerParams(
+            collective_id=0, has_side_effects=True, vmem_limit_bytes=40 * 1024 * 1024
         ),
-        name="suffix",
-    )(suffix_len, query_heads, suffix_cache)
+        name="gather",
+    )(suffix_len, prefix_cache, query_heads, suffix_cache)
 
 
 def prefix_kernel(
@@ -255,13 +466,11 @@
 def gather_plan(queries, prefix_cache, suffix_cache, w_uv, fork_prompt, prompt_slot, suffix_len):
     forks_here = queries.shape[0]
     heads_here = w_uv.shape[0]
-    owners_count = lax.axis_size("dp")
-    tp_count = lax.axis_size("tp")
-    caches = lax.all_gather(prefix_cache[0], ("dp", "tp"), axis=0)
-    caches = caches.reshape(owners_count, tp_count, *prefix_cache.shape[1:])
     starts, order = fork_order(fork_prompt, prompt_slot)
     query_heads = queries.reshape(forks_here, heads_here, R + P_SIZE)
-    latent_suffix, mass_suffix = suffix_attention(query_heads, suffix_cache, suffix_len)
+    caches, latent_suffix, mass_suffix = gather_and_suffix(
+        prefix_cache, query_heads, suffix_cache, suffix_len
+    )
     latent = prefix_attention(starts, order, query_heads, caches, latent_suffix, mass_suffix)
     return project(latent, w_uv).reshape(forks_here, heads_here * V)
 
@@ -272,7 +481,8 @@
     capacity = max(2, 2 * forks_here // owners_count)
     sent = owners_count * capacity * queries.shape[1]
     gathered = owners_count * lax.axis_size("tp") * prefix_cache.size
-    plan = gather_plan if gathered <= 4 * sent else exchange_plan
+    square = lax.axis_size("tp") == 4 and owners_count % 2 == 0
+    plan = gather_plan if square and gathered <= 4 * sent else exchange_plan
     return plan(queries, prefix_cache, *others)
 
 

time: 123 us -> 73.9 us (0.60)
  the two profiles are of different devices: /device:TPU:0 before, /device:TPU:19 now
where the time goes in v2:
time: 73.9 us; the launch traced here: 73.7 us
  Pallas kernels  64.5 us (87%)
  local copies, waits for them, and re-layouts  5.42 us (7%)
  matrix products  2.52 us (3%)
  other arithmetic  1.21 us (2%)
    pallas_call x1, Pallas kernels, gather_and_suffix(): pl.pallas_call(functools.partial(gather_kernel, planes, steps), in_specs=...  48.2 us
    pallas_call x1, Pallas kernels, prefix_attention(): pl.pallas_call(functools.partial(prefix_kernel, group), grid_spec=pltpu.P...  16.2 us
    reshape x1, local copies, waits for them, and re-layouts, gather_plan(): query_heads = queries.reshape(forks_here, heads_here, R + P_SIZE)  4.5 us
    dot_general x1, matrix products, project(): jnp.einsum('nhr,hrv->nhv', latent, w_uv, preferred_element_type=jnp.float32)  2.52 us

profile of v2, /device:TPU:19, one launch (start us, length us, event | category | flops | bytes accessed | tf_op | source)
XLA Modules:
  0.0 73.7 jit_solution(16277888941109414312)
XLA Ops:
  0.0 0.0 copy-start.2
  0.0 0.0 copy-start.1
  0.0 0.8 %select_reduce_fusion.1 = s32[64]{0:T(128)S(1)} fusion(s32[8]{0:T(128)} %param.12, s32[64]{0:T(128)} %bitcast.8), kind=kLoop, calls=%fused_computation.10 | loop fusion | flops 1472 | bytes 544 | tf_op jit(solution)/shard_map/reduce_sum | solution.py:456
  0.8 0.1 convert_reduce_fusion.1.starts_ref
  0.9 0.2 convert_reduce_fusion
  1.1 0.1 select_reduce_fusion.order_ref
  1.2 4.5 %reshape.23.q_ref = bf16[64,32,576]{2,1,0:T(8,128)(2,1)S(1)} reshape(bf16[64,18432]{1,0:T(8,128)(2,1)} %param.7) | data formatting | bytes 4718592 | tf_op jit(solution)/shard_map/reshape | solution.py:470
  5.7 0.0 copy-done.2
  5.7 0.0 copy-done.1
  5.8 0.0 copy-start
  5.8 48.2 %gather.1 = (bf16[8,4,576,256]{3,2,1,0:T(8,128)(2,1)}, bf16[64,32,512]{2,1,0:T(8,128)(2,1)S(1)}, f32[64,32,128]{2,1,0:T(8,128)S(1)}) custom-call(s32[64]{0:T(128)S(1)} %copy-done.2, bf16[1,576,256]{2,1,0:T(8,128)(2,1)S(1)} %copy-done.1, bf16[64,32,576]{2,1,0:T(8,128)(2,1)S(1)} %reshape.23.q_ref, bf16[64,576,128]{2,1,0:T(8,128)(2,1)} %suffix_ref.1), custom_call_target="tpu_custom_call" | custom-call | tf_op jit(solution)/shard_map/gather/pallas_call | solution.py:352
  54.0 0.0 copy-done
  54.0 0.0 copy-start.3
  54.0 16.2 %prefix.1 = bf16[64,32,512]{2,1,0:T(8,128)(2,1)S(1)} custom-call(s32[9]{0:T(128)S(1)} %convert_reduce_fusion.1.starts_ref, s32[64]{0:T(128)S(1)} %select_reduce_fusion.order_ref, bf16[64,32,576]{2,1,0:T(8,128)(2,1)} %copy-done, bf16[8,4,576,256]{3,2,1,0:T(8,128)(2,1)} %get-tuple-element.8.cache_ref, bf16[64,32,512]{2,1,0:T(8,128)(2,1)S(1)} %get-tuple-element.9.latent_ref, ...), custom_call_target="tpu_custom_call" | custom-call | flops 4563402752 | bytes 11796480 | tf_op jit(solution)/shard_map/prefix/pallas_call | solution.py:428
  70.3 0.0 copy-done.3
  70.3 2.5 %fusion.5 = bf16[32,8,8,128]{3,2,1,0:T(8,128)(2,1)S(1)} fusion(bf16[32,512,128]{2,1,0:T(8,128)(2,1)S(1)} %copy-done.3, bf16[64,32,512]{2,1,0:T(8,128)(2,1)S(1)} %prefix.1), kind=kOutput, calls=%fused_computation.3 | convolution fusion | flops 268697600 | bytes 6815744 | tf_op jit(solution)/shard_map/nhr,hrv->nhv/dot_general | solution.py:21
  72.8 0.9 %copy.21 = bf16[32,8,8,128]{3,2,0,1:T(8,128)(2,1)} copy(bf16[32,8,8,128]{3,2,1,0:T(8,128)(2,1)S(1)} %fusion.5) | data formatting | bytes 1048576 | tf_op jit(solution)/shard_map/reshape | solution.py:475
  (1 shorter events, 0.0 us)
Async XLA Ops:
  0.0 5.7 %copy-start.2 = (s32[64]{0:T(128)S(1)}, s32[64]{0:T(128)}, u32[]{:S(2)}) copy-start(s32[64]{0:T(128)} %lens_ref.1) | copy-start | bytes 772
  0.0 5.7 %copy-start.1 = (bf16[1,576,256]{2,1,0:T(8,128)(2,1)S(1)}, bf16[1,576,256]{2,1,0:T(8,128)(2,1)}, u32[]{:S(2)}) copy-start(bf16[1,576,256]{2,1,0:T(8,128)(2,1)} %own_ref.1) | copy-start | bytes 884740
  5.8 48.3 %copy-start = (bf16[64,32,576]{2,1,0:T(8,128)(2,1)}, bf16[64,32,576]{2,1,0:T(8,128)(2,1)S(1)}, u32[]{:S(2)}) copy-start(bf16[64,32,576]{2,1,0:T(8,128)(2,1)S(1)} %reshape.23.q_ref) | copy-start | bytes 7077892
  54.0 16.2 %copy-start.3 = (bf16[32,512,128]{2,1,0:T(8,128)(2,1)S(1)}, bf16[32,512,128]{2,1,0:T(8,128)(2,1)}, u32[]{:S(2)}) copy-start(bf16[32,512,128]{2,1,0:T(8,128)(2,1)} %param.10) | copy-start | bytes 12582916

commit v3 on v2

--- a/solution.py
+++ b/solution.py
@@ -1,4 +1,5 @@
 import functools
+import math
 
 import jax
 import jax.numpy as jnp
@@ -133,13 +134,55 @@
     mass_ref[i] = jnp.broadcast_to(peak + jnp.log(mass), mass_ref.shape[1:])
 
 
+def prefix_group(
+    slot, first, group, ids_ref, q_ref, cache_ref, latent_ref, mass_ref, out_ref
+):
+    heads = q_ref.shape[1]
+    parts = cache_ref.shape[1]
+    ids = [ids_ref[first + i] for i in range(group)]
+    rows = jnp.concatenate([q_ref[fork] for fork in ids], axis=0)
+    scores = [
+        jnp.dot(rows, cache_ref[slot, k], preferred_element_type=jnp.float32)
+        for k in range(parts)
+    ]
+    peak = functools.reduce(
+        jnp.maximum, [jnp.max(piece, axis=1, keepdims=True) for piece in scores]
+    )
+    mass = 0.0
+    summed = 0.0
+    for k in range(parts):
+        weights = jnp.exp2((scores[k] - peak) * (score_scale * log2e))
+        mass = mass + jnp.sum(weights, axis=1, keepdims=True)
+        summed = summed + lax.dot_general(
+            weights.astype(jnp.bfloat16),
+            cache_ref[slot, k, :R, :],
+            OUTER,
+            preferred_element_type=jnp.float32,
+        )
+    peak = peak * score_scale
+    for i, fork in enumerate(ids):
+        own = slice(i * heads, (i + 1) * heads)
+        other = mass_ref[fork][:, :1]
+        top = jnp.maximum(peak[own], other)
+        ours = jnp.exp(peak[own] - top)
+        theirs = jnp.exp(other - top)
+        share = 1.0 / (ours * mass[own] + theirs)
+        out_ref[first + i] = (
+            summed[own] * (ours * share)
+            + latent_ref[fork].astype(jnp.float32) * (theirs * share)
+        ).astype(jnp.bfloat16)
+
+
 def gather_kernel(
     planes,
     steps,
+    group,
     lens_ref,
+    ids_ref,
     own_ref,
     q_ref,
     suffix_ref,
+    packed_ref,
     out_ref,
     latent_ref,
     mass_ref,
@@ -306,20 +349,45 @@
         dx_copy(zz).wait_recv()
         pair_copy(zz, 1 - x, 1 - y).start()
 
-    marks = [steps * r // planes for r in range(planes + 1)]
-    for r in range(planes):
-        if r > 0:
-            arrived(r)
+    capacity = packed_ref.shape[0] // (planes * 2)
+    groups = capacity // group
+
+    def attend(zz):
+        for xx in range(2):
+            for yy in range(2):
+                pair_copy(zz, xx, yy).wait_recv()
+
+        def one(j, carry):
+            slot = zz * 2 + j // groups
+            first = slot * capacity + lax.rem(j, groups) * group
+            prefix_group(
+                slot, first, group, ids_ref, q_ref, out_ref, latent_ref, mass_ref, packed_ref
+            )
+            return carry
+
+        lax.fori_loop(0, 2 * groups, one, 0)
+
+    marks = [min(steps, 3 * r * steps // 8) for r in range(planes + 1)]
+    marks[planes - 1 :] = [steps, steps]
+    compute(0, marks[1])
+    for r in range(1, planes):
+        arrived(r)
+        if r < planes - 1:
             each(r - 1, across)
-        if r > 1:
-            each(r - 2, diagonal)
-        compute(marks[r], marks[r + 1])
-    each(planes - 1, across)
-    if planes > 1:
-        each(planes - 2, diagonal)
-    each(planes - 1, diagonal)
-
+            compute(marks[r], marks[r + 1])
+    compute(marks[planes - 1], steps)
     local.wait()
+    each(0, diagonal)
+    attend(z)
+    for r in range(planes - 2, planes):
+        each(r, across)
+        if r < planes - 1:
+            for d in range(1, r):
+                each(d, diagonal)
+    for d in range(1, planes):
+        if d >= planes - 2:
+            each(d, diagonal)
+        each(d, attend)
 
     @pl.when(has_down)
     def _():
@@ -338,27 +406,29 @@
         dy_copy(zz).wait_send()
         for xx in range(2):
             for yy in range(2):
-                pair_copy(zz, xx, yy).wait()
-
-
-def gather_and_suffix(prefix_cache, query_heads, suffix_cache, suffix_len, steps=8):
+                pair_copy(zz, xx, yy).wait_send()
+
+
+def gather_and_attend(
+    prefix_cache, query_heads, suffix_cache, suffix_len, ids, steps=8
+):
     forks, heads, width = query_heads.shape
-    keys = suffix_cache.shape[2]
     slots, parts = lax.axis_size("dp"), lax.axis_size("tp")
     planes = slots // 2
+    group = math.gcd(8, ids.shape[0] // slots)
     dma = pltpu.SemaphoreType.DMA
+    smem = pl.BlockSpec(memory_space=pltpu.SMEM)
     vmem = pl.BlockSpec(memory_space=pltpu.VMEM)
     hbm = pl.BlockSpec(memory_space=pl.ANY)
     return pl.pallas_call(
-        functools.partial(gather_kernel, planes, steps),
-        in_specs=[pl.BlockSpec(memory_space=pltpu.SMEM), hbm, vmem, hbm],
-        out_specs=[hbm, vmem, vmem],
-        out_shape=[
-            jax.ShapeDtypeStruct((slots, parts, *prefix_cache.shape[1:]), jnp.bfloat16),
-            jax.ShapeDtypeStruct((forks, heads, R), jnp.bfloat16),
-            jax.ShapeDtypeStruct((forks, heads, 128), jnp.float32),
-        ],
+        functools.partial(gather_kernel, planes, steps, group),
+        in_specs=[smem, smem, hbm, vmem, hbm],
+        out_specs=vmem,
+        out_shape=jax.ShapeDtypeStruct((ids.shape[0], heads, R), jnp.bfloat16),
         scratch_shapes=[
+            pltpu.VMEM((slots, parts, *prefix_cache.shape[1:]), jnp.bfloat16),
+            pltpu.VMEM((forks, heads, R), jnp.bfloat16),
+            pltpu.VMEM((forks, heads, 128), jnp.float32),
             pltpu.VMEM(suffix_cache.shape, jnp.bfloat16),
             dma((steps,)),
             dma,
@@ -368,110 +438,50 @@
             dma((slots * 2,)),
         ],
         compiler_params=pltpu.CompilerParams(
-            collective_id=0, has_side_effects=True, vmem_limit_bytes=40 * 1024 * 1024
+            collective_id=0, has_side_effects=True, vmem_limit_bytes=48 * 1024 * 1024
         ),
         name="gather",
-    )(suffix_len, prefix_cache, query_heads, suffix_cache)
-
-
-def prefix_kernel(
-    group, starts_ref, order_ref, q_ref, cache_ref, latent_ref, mass_ref, out_ref
-):
-    slot = pl.program_id(0)
-    heads = q_ref.shape[1]
-    first = starts_ref[slot]
-    last = starts_ref[slot + 1] - 1
-    parts = cache_ref.shape[1]
-
-    def one_group(g, carry):
-        ids = [order_ref[jnp.minimum(first + g * group + i, last)] for i in range(group)]
-        rows = jnp.concatenate([q_ref[fork] for fork in ids], axis=0)
-        scores = [
-            jnp.dot(rows, cache_ref[0, k], preferred_element_type=jnp.float32)
-            for k in range(parts)
-        ]
-        peak = functools.reduce(
-            jnp.maximum, [jnp.max(piece, axis=1, keepdims=True) for piece in scores]
-        )
-        mass = 0.0
-        summed = 0.0
-        for k in range(parts):
-            weights = jnp.exp2((scores[k] - peak) * (score_scale * log2e))
-            mass = mass + jnp.sum(weights, axis=1, keepdims=True)
-            summed = summed + lax.dot_general(
-                weights.astype(jnp.bfloat16),
-                cache_ref[0, k, :R, :],
-                OUTER,
-                preferred_element_type=jnp.float32,
-            )
-        peak = peak * score_scale
-        for i, fork in enumerate(ids):
-            own = slice(i * heads, (i + 1) * heads)
-            other = mass_ref[fork][:, :1]
-            top = jnp.maximum(peak[own], other)
-            ours = jnp.exp(peak[own] - top)
-            theirs = jnp.exp(other - top)
-            share = 1.0 / (ours * mass[own] + theirs)
-            out_ref[fork] = (
-                summed[own] * (ours * share)
-                + latent_ref[fork].astype(jnp.float32) * (theirs * share)
-            ).astype(jnp.bfloat16)
-        return carry
-
-    lax.fori_loop(0, (last - first + group) // group, one_group, 0)
-
-
-def prefix_attention(starts, order, query_heads, caches, latent_suffix, mass_suffix, group=8):
-    forks, heads, width = query_heads.shape
-    slots, parts, _, keys = caches.shape
-    whole = lambda s, a, b: (0, 0, 0)
+    )(suffix_len, ids, prefix_cache, query_heads, suffix_cache)
+
+
+def unpack_kernel(target_ref, packed_ref, out_ref):
+    for fork in range(out_ref.shape[0]):
+        out_ref[fork] = packed_ref[target_ref[fork]]
+
+
+def unpack(target, packed):
+    vmem = pl.BlockSpec(memory_space=pltpu.VMEM)
     return pl.pallas_call(
-        functools.partial(prefix_kernel, group),
-        grid_spec=pltpu.PrefetchScalarGridSpec(
-            num_scalar_prefetch=2,
-            grid=(slots,),
-            in_specs=[
-                pl.BlockSpec((forks, heads, width), whole),
-                pl.BlockSpec((1, parts, width, keys), lambda s, a, b: (s, 0, 0, 0)),
-                pl.BlockSpec((forks, heads, R), whole),
-                pl.BlockSpec((forks, heads, 128), whole),
-            ],
-            out_specs=pl.BlockSpec((forks, heads, R), whole),
-        ),
-        out_shape=jax.ShapeDtypeStruct((forks, heads, R), jnp.bfloat16),
-        cost_estimate=pl.CostEstimate(
-            flops=2 * forks * heads * parts * keys * (width + R),
-            bytes_accessed=2 * caches.size + 2 * query_heads.size,
-            transcendentals=forks * heads * parts * keys,
-        ),
-        compiler_params=pltpu.CompilerParams(vmem_limit_bytes=48 * 1024 * 1024),
-        name="prefix",
-    )(starts, order, query_heads, caches, latent_suffix, mass_suffix)
-
-
-def fork_order(fork_prompt, prompt_slot):
+        unpack_kernel,
+        in_specs=[pl.BlockSpec(memory_space=pltpu.SMEM), vmem],
+        out_specs=vmem,
+        out_shape=jax.ShapeDtypeStruct((target.shape[0], *packed.shape[1:]), packed.dtype),
+        name="unpack",
+    )(target, packed)
+
+
+def fork_places(fork_prompt, prompt_slot, slots, capacity):
     forks = fork_prompt.shape[0]
     prompt_ids = jnp.arange(prompt_slot.shape[0], dtype=jnp.int32)
     chosen = fork_prompt[:, 0][:, None] == prompt_ids[None, :]
     owner_slot = jnp.sum(jnp.where(chosen, prompt_slot[None, :], 0), axis=1)
-    ids = jnp.arange(forks, dtype=jnp.int32)
-    key = owner_slot * forks + ids
-    place = jnp.sum((key[None, :] < key[:, None]).astype(jnp.int32), axis=1)
-    order = jnp.sum(jnp.where(place[None, :] == ids[:, None], ids[None, :], 0), axis=1)
-    edges = jnp.arange(prompt_slot.shape[0] + 1, dtype=jnp.int32)
-    starts = jnp.sum((owner_slot[None, :] < edges[:, None]).astype(jnp.int32), axis=1)
-    return starts, order
+    order = jnp.arange(forks, dtype=jnp.int32)
+    before = (owner_slot[:, None] == owner_slot[None, :]) & (order[None, :] < order[:, None])
+    target = owner_slot * capacity + jnp.sum(before.astype(jnp.int32), axis=1)
+    spots = jnp.arange(slots * capacity, dtype=jnp.int32)
+    ids = jnp.sum(jnp.where(target[None, :] == spots[:, None], order[None, :], 0), axis=1)
+    return target, ids
 
 
 def gather_plan(queries, prefix_cache, suffix_cache, w_uv, fork_prompt, prompt_slot, suffix_len):
     forks_here = queries.shape[0]
     heads_here = w_uv.shape[0]
-    starts, order = fork_order(fork_prompt, prompt_slot)
+    slots = lax.axis_size("dp")
+    capacity = max(2, 2 * forks_here // slots)
+    target, ids = fork_places(fork_prompt, prompt_slot, slots, capacity)
     query_heads = queries.reshape(forks_here, heads_here, R + P_SIZE)
-    caches, latent_suffix, mass_suffix = gather_and_suffix(
-        prefix_cache, query_heads, suffix_cache, suffix_len
-    )
-    latent = prefix_attention(starts, order, query_heads, caches, latent_suffix, mass_suffix)
+    packed = gather_and_attend(prefix_cache, query_heads, suffix_cache, suffix_len, ids)
+    latent = unpack(target, packed)
     return project(latent, w_uv).reshape(forks_here, heads_here * V)
 
 

time: 73.9 us -> 74.4 us (level)
  the two profiles are of different devices: /device:TPU:19 before, /device:TPU:0 now
where the time goes in v3:
time: 74.4 us; the launch traced here: 74.2 us
  Pallas kernels  62.3 us (84%)
  local copies, waits for them, and re-layouts  5.39 us (7%)
  matrix products  5.34 us (7%)
  other arithmetic  1.08 us (1%)
    pallas_call x1, Pallas kernels, gather_and_attend(): pl.pallas_call(functools.partial(gather_kernel, planes, steps, group), in...  58.7 us
    dot_general x1, matrix products, project(): jnp.einsum('nhr,hrv->nhv', latent, w_uv, preferred_element_type=jnp.float32)  5.34 us
    reshape x1, local copies, waits for them, and re-layouts, gather_plan(): query_heads = queries.reshape(forks_here, heads_here, R + P_SIZE)  4.48 us
    pallas_call x1, Pallas kernels, unpack(): pl.pallas_call(unpack_kernel, in_specs=[pl.BlockSpec(memory_space=pltpu.S...  3.67 us

profile of v3, /device:TPU:0, one launch (start us, length us, event | category | flops | bytes accessed | tf_op | source)
XLA Modules:
  0.0 74.2 jit_solution(16471164159325657115)
XLA Ops:
  0.0 0.0 copy-start.1
  0.0 0.0 copy-start
  0.0 0.8 %select_reduce_fusion.1 = s32[64]{0:T(128)S(1)} fusion(s32[8]{0:T(128)} %param.12, s32[64]{0:T(128)} %bitcast.8), kind=kLoop, calls=%fused_computation.10 | loop fusion | flops 1472 | bytes 544 | tf_op jit(solution)/shard_map/reduce_sum | solution.py:467
  0.8 0.2 convert_reduce_fusion
  1.0 0.0 copy-start.2
  1.0 0.1 select_reduce_fusion.ids_ref
  1.1 4.5 %reshape.15.q_ref = bf16[64,32,576]{2,1,0:T(8,128)(2,1)S(1)} reshape(bf16[64,18432]{1,0:T(8,128)(2,1)} %param.7) | data formatting | bytes 4718592 | tf_op jit(solution)/shard_map/reshape | solution.py:482
  5.6 0.0 copy-done.1
  5.6 0.0 copy-done
  5.6 58.7 %gather.1.packed_ref = bf16[128,32,512]{2,1,0:T(8,128)(2,1)} custom-call(s32[64]{0:T(128)S(1)} %copy-done.1, s32[128]{0:T(128)S(1)} %select_reduce_fusion.ids_ref, bf16[1,576,256]{2,1,0:T(8,128)(2,1)S(1)} %copy-done, bf16[64,32,576]{2,1,0:T(8,128)(2,1)S(1)} %reshape.15.q_ref, bf16[64,576,128]{2,1,0:T(8,128)(2,1)} %suffix_ref.1), custom_call_target="tpu_custom_call" | custom-call | tf_op jit(solution)/shard_map/gather/pallas_call | solution.py:423
  64.3 0.0 copy-done.2
  64.3 3.7 %unpack.1 = bf16[64,32,512]{2,1,0:T(8,128)(2,1)} custom-call(s32[64]{0:T(128)} %copy-done.2, bf16[128,32,512]{2,1,0:T(8,128)(2,1)} %gather.1.packed_ref), custom_call_target="tpu_custom_call" | custom-call | tf_op jit(solution)/shard_map/unpack/pallas_call | solution.py:454
  68.0 5.3 %fusion.5 = bf16[32,8,8,128]{3,2,1,0:T(8,128)(2,1)S(1)} fusion(bf16[32,512,128]{2,1,0:T(8,128)(2,1)} %param.10, bf16[64,32,512]{2,1,0:T(8,128)(2,1)} %unpack.1), kind=kOutput, calls=%fused_computation.3 | convolution fusion | flops 268697600 | bytes 6815744 | tf_op jit(solution)/shard_map/nhr,hrv->nhv/dot_general | solution.py:22
  73.3 0.9 %copy.21 = bf16[32,8,8,128]{3,2,0,1:T(8,128)(2,1)} copy(bf16[32,8,8,128]{3,2,1,0:T(8,128)(2,1)S(1)} %fusion.5) | data formatting | bytes 1048576 | tf_op jit(solution)/shard_map/reshape | solution.py:485
  (1 shorter events, 0.0 us)
Async XLA Ops:
  0.0 5.6 %copy-start.1 = (s32[64]{0:T(128)S(1)}, s32[64]{0:T(128)}, u32[]{:S(2)}) copy-start(s32[64]{0:T(128)} %lens_ref.1) | copy-start | bytes 772
  0.0 5.6 %copy-start = (bf16[1,576,256]{2,1,0:T(8,128)(2,1)S(1)}, bf16[1,576,256]{2,1,0:T(8,128)(2,1)}, u32[]{:S(2)}) copy-start(bf16[1,576,256]{2,1,0:T(8,128)(2,1)} %own_ref.1) | copy-start | bytes 884740
  1.0 63.3 %copy-start.2 = (s32[64]{0:T(128)}, s32[64]{0:T(128)S(1)}, u32[]{:S(2)}) copy-start(s32[64]{0:T(128)S(1)} %multiply_add_fusion.target_ref) | copy-start | bytes 772
